TPU v7x, 256 devices: a whole 4x4x8 slice. The times are simulated.
256 devices in a mesh: fsdp: 64 (over z, y, core), rep: 4 (over x).
Axes of the slice: x: 4, y: 4, z: 8, core: 2. Of those that a mesh axis runs over, the one named last changes fastest.
Arguments:
- partial_grad: bfloat16 [4, 64, 1024, 1024], P('rep', None, 'fsdp'), may hold values from -3 to 3
- owner_table: int32 [64, 2], replicated, may hold values from -1 to 63, as said below
- left_stat: float32 [64, 2, 1024, 1024], P('fsdp', None, None, 'rep'), may hold values from -6 to 6
- right_stat: float32 [64, 2, 1024, 1024], P('fsdp', None, None, 'rep'), may hold values from -6 to 6
- left_root: bfloat16 [64, 2, 1024, 1024], P('fsdp', None, None, 'rep'), may hold values from -0.1875 to 0.1875
- right_root: bfloat16 [64, 2, 1024, 1024], P('fsdp', None, None, 'rep'), may hold values from -0.1875 to 0.1875
Outputs:
- left_new: float32 [64, 2, 1024, 1024], P('fsdp', None, None, 'rep')
- right_new: float32 [64, 2, 1024, 1024], P('fsdp', None, None, 'rep')
- update: bfloat16 [64, 1024, 1024], P(None, 'fsdp', 'rep')
Inputs may be any that keep to these rules, and one draw needn't show every extreme that they name: `owner_table`: each of the 64 blocks stands in exactly one slot and -1 marks an empty slot; some owner fills all 2 slots and some owner has none.
All inputs are finite; a program needn't handle non-finite values.
Results may differ from a plain program's by a relative error of at most 0.014.
Values may be sent and summed in bfloat16 or wider, within the bound.
A program may use at most 64 MiB of HBM per device.

v0:
```python
import jax
import jax.numpy as jnp
from jax import lax
from jax.sharding import PartitionSpec as P

decay_rate = 0.99


def in_blocks(x, dim, size):
    shape = x.shape
    parts = x.reshape(*shape[:dim], size, shape[dim] // size, *shape[dim + 1 :])
    return jnp.moveaxis(parts, dim, 0)


def summed_on_arrival(x, axis, dim):
    size = lax.axis_size(axis)
    parts = lax.all_to_all(in_blocks(x, dim, size), axis, 0, 0, tiled=True)
    return jnp.sum(parts.astype(jnp.float32), axis=0)


def on_device(partial_grad, owner_table, left_stat, right_stat, left_root, right_root):
    local_grad = partial_grad[0]
    block_count = local_grad.shape[0]
    my_row = lax.dynamic_index_in_dim(owner_table, lax.axis_index("fsdp"), 0, keepdims=False)
    is_filled = my_row >= 0
    sender_index = jnp.maximum(owner_table.T, 0)
    sender_mask = owner_table.T >= 0
    shares = summed_on_arrival(
        local_grad.astype(jnp.float32).astype(jnp.bfloat16), "rep", 2
    ).astype(jnp.bfloat16)
    picked = jnp.take(shares, sender_index, axis=0)
    picked = jnp.where(sender_mask[:, :, None, None], picked, jnp.zeros((), picked.dtype))
    columns = lax.all_to_all(
        picked.reshape(picked.shape[0], -1, picked.shape[3]),
        "fsdp",
        split_axis=1,
        concat_axis=1,
        tiled=True,
    )
    gradient = lax.all_gather(columns, "rep", axis=2, tiled=True)
    share_width = left_stat.shape[3]
    first_col = lax.axis_index("rep") * share_width
    rows_share = lax.dynamic_slice_in_dim(gradient, first_col, share_width, 1)
    cols_share = lax.dynamic_slice_in_dim(gradient, first_col, share_width, 2)
    left_term = jnp.einsum("sik,sjk->sij", gradient, rows_share, preferred_element_type=jnp.float32)
    right_term = jnp.einsum(
        "ski,skj->sij", gradient, cols_share, preferred_element_type=jnp.float32
    )
    keeper = is_filled[:, None, None]
    left_next = jnp.where(
        keeper, decay_rate * left_stat[0] + (1.0 - decay_rate) * left_term, left_stat[0]
    )
    right_next = jnp.where(
        keeper, decay_rate * right_stat[0] + (1.0 - decay_rate) * right_term, right_stat[0]
    )
    applied = jnp.einsum(
        "sik,skj->sij",
        lax.all_gather(left_root[0], "rep", axis=2, tiled=True),
        gradient,
        preferred_element_type=jnp.float32,
    ).astype(jnp.bfloat16)
    result_cols = jnp.einsum(
        "sik,skj->sij", applied, right_root[0], preferred_element_type=jnp.float32
    ).astype(jnp.bfloat16)
    returned = lax.all_to_all(result_cols, "fsdp", split_axis=1, concat_axis=0, tiled=True)
    flat_table = owner_table.reshape(-1)
    slot_ids = jnp.arange(flat_table.shape[0], dtype=jnp.int32)
    block_ids = jnp.arange(block_count, dtype=jnp.int32)
    positions = jnp.sum(
        jnp.where(flat_table[None, :] == block_ids[:, None], slot_ids[None, :], 0), axis=1
    )
    update = jnp.take(returned, positions, axis=0)
    return (left_next[None], right_next[None], update)


def solution(mesh):
    return jax.shard_map(
        on_device,
        mesh=mesh,
        in_specs=(
            P("rep", None, "fsdp", None),
            P(),
            P("fsdp", None, None, "rep"),
            P("fsdp", None, None, "rep"),
            P("fsdp", None, None, "rep"),
            P("fsdp", None, None, "rep"),
        ),
        out_specs=(
            P("fsdp", None, None, "rep"),
            P("fsdp", None, None, "rep"),
            P(None, "fsdp", "rep"),
        ),
        check_vma=False,
    )
```

profile of v0, /device:TPU:1, one launch (start us, length us, event | category | flops | bytes accessed | tf_op | source)
XLA Modules:
  0.0 213.5 jit_solution(4872526677755833323)
XLA Ops:
  7.2 0.7 all-gather.6.cloned.1.call-update
  7.9 3.3 %reshape.46 = bf16[64,16,4,256]{3,2,1,0:T(4,128)(2,1)S(1)} reshape(bf16[1,64,16,1024]{3,2,1,0:T(8,128)(2,1)} %param.6) | data formatting | bytes 4194304 | tf_op jit(solution)/shard_map/reshape | solution.py:11
  11.3 1.6 copy.32
  12.9 5.0 %all-to-all-start = ((bf16[4,64,16,256]{3,2,1,0:T(8,128)(2,1)}), bf16[4,64,16,256]{3,2,1,0:T(8,128)(2,1)S(1)}, u32[]{:S(2)}, u32[]{:S(2)}) async-start(bf16[4,64,16,256]{3,2,1,0:T(8,128)(2,1)} %copy.32), calls=%async_computation | async-start | bytes 4194304 | tf_op jit(solution)/shard_map/all_to_all | solution.py:17
  18.4 35.2 %all-to-all-done = bf16[4,64,16,256]{3,2,1,0:T(8,128)(2,1)S(1)} async-done(((bf16[4,64,16,256]{3,2,1,0:T(8,128)(2,1)}), bf16[4,64,16,256]{3,2,1,0:T(8,128)(2,1)S(1)}, u32[]{:S(2)}, u32[]{:S(2)}) %all-to-all-start) | async-done | bytes 2097184 | tf_op jit(solution)/shard_map/all_to_all | solution.py:17
  53.5 1.2 reduce_sum.23
  54.8 1.7 gather_fusion
  56.5 0.9 fusion.18
  57.4 1.1 copy.33
  58.5 42.5 %all_to_all.28 = bf16[2,1024,256]{2,0,1:T(2,128)(2,1)S(1)} all-to-all(bf16[2,1024,256]{2,0,1:T(2,128)(2,1)S(1)} %copy.33), channel_id=1, replica_groups=mesh['fsdp'=64,'rep'=4] {'fsdp'}, dimensions={1} | all-to-all | bytes 2097152 | tf_op jit(solution)/shard_map/all_to_all | solution.py:33
  101.0 1.1 copy.34
  102.2 50.5 %all-gather.4.cloned.1.call-done = bf16[2,1024,1024]{2,1,0:T(8,128)(2,1)} async-done(((bf16[2,1024,256]{2,1,0:T(8,128)(2,1)}), bf16[2,1024,1024]{2,1,0:T(8,128)(2,1)}) %all-gather.4.cloned.1.call-update) | async-done | bytes 4194320 | tf_op jit(solution)/shard_map/all_gather | solution.py:40
  152.7 9.9 %fusion.12 = bf16[2,1024,256]{2,1,0:T(8,128)(2,1)S(1)} fusion(bf16[2,1024,1024]{2,1,0:T(8,128)(2,1)} %all-gather.4.cloned.1.call-done, bf16[1,2,1024,1024]{3,2,1,0:T(8,128)(2,1)} %all-gather.6.cloned.1.call-done, bf16[1,2,1024,256]{3,2,1,0:T(8,128)(2,1)S(1)} %copy-done), kind=kOutput, calls=%fused_computation.14 | convolution fusion | flops 5371330560 | bytes 10485760 | tf_op jit(solution)/shard_map/sik,skj->sij/dot_general | solution.py:62
  162.5 2.1 copy.39
  164.6 12.1 %all-to-all-start.2 = ((bf16[2,1024,256]{2,0,1:T(2,128)(2,1)}), bf16[2,1024,256]{2,0,1:T(2,128)(2,1)S(1)}, u32[]{:S(2)}, u32[]{:S(2)}) async-start(bf16[2,1024,256]{2,0,1:T(2,128)(2,1)} %copy.39), calls=%async_computation.2 | async-start | bytes 2097152 | tf_op jit(solution)/shard_map/all_to_all | solution.py:65
  176.8 0.1 eq.15
  176.9 0.2 compare_reduce_fusion
  177.3 6.4 %fusion.5 = f32[1,2,1024,256]{3,2,1,0:T(8,128)} fusion(f32[1,2,1024,256]{3,2,1,0:T(8,128)} %param.9, bf16[2,1024,1024]{2,1,0:T(8,128)(2,1)} %all-gather.4.cloned.1.call-done, s32[]{:T(128)S(6)} %select_n.55, pred[2]{0:T(512)(128)(4,1)S(1)} %compare_reduce_fusion), kind=kOutput, calls=%fused_computation.9 | convolution fusion | flops 1075838976 | bytes 9437190 | tf_op jit(solution)/shard_map/ski,skj->sij/dot_general | solution.py:46
  183.7 2.7 %fusion.7 = f32[1,2,1024,256]{3,2,1,0:T(8,128)} fusion(f32[1,2,1024,256]{3,2,1,0:T(8,128)S(1)} %copy-done.3, bf16[2,1024,1024]{2,1,0:T(8,128)(2,1)S(1)} %copy-done.2, s32[]{:T(128)S(6)} %select_n.55, pred[2]{0:T(512)(128)(4,1)S(1)} %compare_reduce_fusion), kind=kOutput, calls=%fused_computation.13 | convolution fusion | flops 1075838976 | bytes 9437700 | tf_op jit(solution)/shard_map/sik,sjk->sij/dot_general | solution.py:45
  186.5 18.4 %all-to-all-done.2 = bf16[2,1024,256]{2,0,1:T(2,128)(2,1)S(1)} async-done(((bf16[2,1024,256]{2,0,1:T(2,128)(2,1)}), bf16[2,1024,256]{2,0,1:T(2,128)(2,1)S(1)}, u32[]{:S(2)}, u32[]{:S(2)}) %all-to-all-start.2) | async-done | bytes 1048608 | tf_op jit(solution)/shard_map/all_to_all | solution.py:65
  204.8 0.1 copy.40
  205.0 0.1 copy.41
  205.1 0.6 gather_fusion.1
  205.7 0.9 broadcast_select_fusion
  (26 shorter events, 0.8 us)
Async XLA Ops:
  7.2 145.5 %copy-start = (bf16[1,2,1024,256]{3,2,1,0:T(8,128)(2,1)S(1)}, bf16[1,2,1024,256]{3,2,1,0:T(8,128)(2,1)}, u32[]{:S(2)}) copy-start(bf16[1,2,1024,256]{3,2,1,0:T(8,128)(2,1)} %param.11) | copy-start | bytes 3145732
  7.2 95.0 %all-gather.6.cloned.1.call-start = ((), (), s32[]{:S(2)}) async-start(), calls=%async_computation.4 | async-start | bytes 5242880 | tf_op jit(solution)/shard_map/all_gather | solution.py:58
  12.9 5.0 %copy-start.1 = (s32[64,2]{0,1:T(2,128)S(1)}, s32[64,2]{0,1:T(2,128)}, u32[]{:S(2)}) copy-start(s32[64,2]{0,1:T(2,128)} %param.7) | copy-start | bytes 1540
  12.9 40.7 %all-to-all-start = ((bf16[4,64,16,256]{3,2,1,0:T(8,128)(2,1)}), bf16[4,64,16,256]{3,2,1,0:T(8,128)(2,1)S(1)}, u32[]{:S(2)}, u32[]{:S(2)}) async-start(bf16[4,64,16,256]{3,2,1,0:T(8,128)(2,1)} %copy.32), calls=%async_computation | async-start | bytes 4194304 | tf_op jit(solution)/shard_map/all_to_all | solution.py:17
  17.8 134.8 %all-gather.4.cloned.1.call-start = ((), (), s32[]{:S(2)}) async-start(), calls=%async_computation.3 | async-start | bytes 5242880 | tf_op jit(solution)/shard_map/all_gather | solution.py:40
  164.6 40.2 %all-to-all-start.2 = ((bf16[2,1024,256]{2,0,1:T(2,128)(2,1)}), bf16[2,1024,256]{2,0,1:T(2,128)(2,1)S(1)}, u32[]{:S(2)}, u32[]{:S(2)}) async-start(bf16[2,1024,256]{2,0,1:T(2,128)(2,1)} %copy.39), calls=%async_computation.2 | async-start | bytes 2097152 | tf_op jit(solution)/shard_map/all_to_all | solution.py:65
  177.2 6.5 %copy-start.2 = (bf16[2,1024,1024]{2,1,0:T(8,128)(2,1)S(1)}, bf16[2,1024,1024]{2,1,0:T(8,128)(2,1)}, u32[]{:S(2)}) copy-start(bf16[2,1024,1024]{2,1,0:T(8,128)(2,1)} %all-gather.4.cloned.1.call-done) | copy-start | bytes 12582916
  177.3 6.5 %copy-start.3 = (f32[1,2,1024,256]{3,2,1,0:T(8,128)S(1)}, f32[1,2,1024,256]{3,2,1,0:T(8,128)}, u32[]{:S(2)}) copy-start(f32[1,2,1024,256]{3,2,1,0:T(8,128)} %param.8) | copy-start | bytes 6291460
Sparse Core Ops, SparseCore 0:
  9.8 70.3 all-gather.5
  102.3 50.3 all-gather.3
where the time goes:
time: 214 us
  waiting for transfers between devices  105 us (49%)
  blocking collectives  42.5 us (20%)
  matrix products  19 us (9%)
  starting transfers between devices  17.1 us (8%)
  between operations  14.2 us (7%)
  local copies, waits for them, and re-layouts  12.5 us (6%)
  other arithmetic  3.46 us (2%)
    all_gather x1, waiting for transfers between devices, on_device(): gradient = lax.all_gather(columns, 'rep', axis=2, tiled=True)  50.5 us
    all_to_all x1, blocking collectives, on_device(): lax.all_to_all(picked.reshape(picked.shape[0], -1, picked.shape[3]), 'fsd...  42.5 us
    all_to_all x1, waiting for transfers between devices, summed_on_arrival(): parts = lax.all_to_all(in_blocks(x, dim, size), axis, 0, 0, tiled=True)  35.2 us
    all_to_all x1, waiting for transfers between devices, on_device(): lax.all_to_all(result_cols, 'fsdp', split_axis=1, concat_axis=0, tiled=True)  18.4 us
    all_to_all x1, starting transfers between devices, on_device(): lax.all_to_all(result_cols, 'fsdp', split_axis=1, concat_axis=0, tiled=True)  12.1 us
    dot_general x1, matrix products, on_device(): jnp.einsum('sik,skj->sij', applied, right_root[0], preferred_element_type...  9.85 us
    dot_general x1, matrix products, on_device(): jnp.einsum('ski,skj->sij', gradient, cols_share, preferred_element_type=j...  6.45 us
    all_to_all x1, starting transfers between devices, summed_on_arrival(): parts = lax.all_to_all(in_blocks(x, dim, size), axis, 0, 0, tiled=True)  4.96 us
  transfers between devices with their start and end apart: 4, of which 3 were waited for; matrix products, arithmetic and copies ran while one was open for 10% of the time, Pallas kernels for 0%

commit v1 on v0

--- a/solution.py
+++ b/solution.py
@@ -37,7 +37,7 @@
         concat_axis=1,
         tiled=True,
     )
-    gradient = lax.all_gather(columns, "rep", axis=2, tiled=True)
+    gradient = jnp.concatenate(lax.all_gather(columns, "rep"), axis=2)
     share_width = left_stat.shape[3]
     first_col = lax.axis_index("rep") * share_width
     rows_share = lax.dynamic_slice_in_dim(gradient, first_col, share_width, 1)

time: 214 us -> 252 us (1.18)
  waiting for transfers between devices: 105 us -> 138 us
  local copies, waits for them, and re-layouts: 12.5 us -> 17.3 us
    all_gather x1, waiting for transfers between devices: 0.02 us -> 50.2 us  [on_device(): lax.all_gather(left_root[0], 'rep', axis=2, tiled=True)]
    all_to_all x1, waiting for transfers between devices: 35.2 us -> 24 us  [summed_on_arrival(): parts = lax.all_to_all(in_blocks(x, dim, size), axis, 0, 0, tiled=True)]
    all_gather x1, waiting for transfers between devices: 50.5 us -> 45 us  [on_device(): gradient = jnp.concatenate(lax.all_gather(columns, 'rep'), axis=2)]
    reshape x0 -> x1, local copies, waits for them, and re-layouts: none -> 4.71 us  [on_device(): gradient = jnp.concatenate(lax.all_gather(columns, 'rep'), axis=2)]
  transfers between devices with their start and end apart: 4 -> 4, of which waited for: 3 -> 4; matrix products, arithmetic and copies ran while one was open for 10% -> 6% of each run, Pallas kernels for 0% -> 0%
where the time goes in v1:
time: 252 us
  waiting for transfers between devices  138 us (55%)
  blocking collectives  42.4 us (17%)
  matrix products  19.1 us (8%)
  local copies, waits for them, and re-layouts  17.3 us (7%)
  starting transfers between devices  17.1 us (7%)
  between operations  14.2 us (6%)
  other arithmetic  3.45 us (1%)
    all_gather x1, waiting for transfers between devices, on_device(): lax.all_gather(left_root[0], 'rep', axis=2, tiled=True)  50.2 us
    all_gather x1, waiting for transfers between devices, on_device(): gradient = jnp.concatenate(lax.all_gather(columns, 'rep'), axis=2)  45 us
    all_to_all x1, blocking collectives, on_device(): lax.all_to_all(picked.reshape(picked.shape[0], -1, picked.shape[3]), 'fsd...  42.4 us
    all_to_all x1, waiting for transfers between devices, summed_on_arrival(): parts = lax.all_to_all(in_blocks(x, dim, size), axis, 0, 0, tiled=True)  24 us
    all_to_all x1, waiting for transfers between devices, on_device(): lax.all_to_all(result_cols, 'fsdp', split_axis=1, concat_axis=0, tiled=True)  18.3 us
    all_to_all x1, starting transfers between devices, on_device(): lax.all_to_all(result_cols, 'fsdp', split_axis=1, concat_axis=0, tiled=True)  12.1 us
    dot_general x1, matrix products, on_device(): jnp.einsum('sik,skj->sij', applied, right_root[0], preferred_element_type...  9.85 us
    dot_general x1, matrix products, on_device(): jnp.einsum('ski,skj->sij', gradient, cols_share, preferred_element_type=j...  6.45 us
  transfers between devices with their start and end apart: 4, of which 4 were waited for; matrix products, arithmetic and copies ran while one was open for 6% of the time, Pallas kernels for 0%

profile of v1, /device:TPU:1, one launch (start us, length us, event | category | flops | bytes accessed | tf_op | source)
XLA Modules:
  0.0 251.7 jit_solution(9658902887312768706)
XLA Ops:
  7.2 3.4 %reshape.52 = bf16[64,16,4,256]{3,2,1,0:T(4,128)(2,1)S(1)} reshape(bf16[1,64,16,1024]{3,2,1,0:T(8,128)(2,1)} %param.6) | data formatting | bytes 4194304 | tf_op jit(solution)/shard_map/reshape | solution.py:11
  10.6 1.6 copy.35
  12.2 5.0 %all-to-all-start = ((bf16[4,64,16,256]{3,2,1,0:T(8,128)(2,1)}), bf16[4,64,16,256]{3,2,1,0:T(8,128)(2,1)S(1)}, u32[]{:S(2)}, u32[]{:S(2)}) async-start(bf16[4,64,16,256]{3,2,1,0:T(8,128)(2,1)} %copy.35), calls=%async_computation | async-start | bytes 4194304 | tf_op jit(solution)/shard_map/all_to_all | solution.py:17
  17.7 24.0 %all-to-all-done = bf16[4,64,16,256]{3,2,1,0:T(8,128)(2,1)S(1)} async-done(((bf16[4,64,16,256]{3,2,1,0:T(8,128)(2,1)}), bf16[4,64,16,256]{3,2,1,0:T(8,128)(2,1)S(1)}, u32[]{:S(2)}, u32[]{:S(2)}) %all-to-all-start) | async-done | bytes 2097184 | tf_op jit(solution)/shard_map/all_to_all | solution.py:17
  41.7 1.2 reduce_sum.23
  42.9 1.7 gather_fusion
  44.6 0.9 fusion.18
  45.5 1.1 copy.36
  46.6 42.4 %all_to_all.28 = bf16[2,1024,256]{2,0,1:T(2,128)(2,1)S(1)} all-to-all(bf16[2,1024,256]{2,0,1:T(2,128)(2,1)S(1)} %copy.36), channel_id=1, replica_groups=mesh['fsdp'=64,'rep'=4] {'fsdp'}, dimensions={1} | all-to-all | bytes 2097152 | tf_op jit(solution)/shard_map/all_to_all | solution.py:33
  89.1 1.1 copy.37
  90.2 0.7 all-gather.7.cloned.1.call-update
  90.9 45.0 %all-gather.5.cloned.1.call-done = bf16[8,1024,256]{2,1,0:T(8,128)(2,1)} async-done(((bf16[2,1024,256]{2,1,0:T(8,128)(2,1)}), bf16[8,1024,256]{2,1,0:T(8,128)(2,1)}) %all-gather.5.cloned.1.call-update) | async-done | bytes 4194320 | tf_op jit(solution)/shard_map/all_gather | solution.py:40
  136.0 4.7 %copy.49 = bf16[4,2,128,8,256]{4,3,0,2,1:T(8,128)(2,1)} copy(bf16[4,2,128,8,256]{4,3,2,1,0:T(8,128)(2,1)} %bitcast.68) | data formatting | bytes 8388608 | tf_op jit(solution)/shard_map/reshape | solution.py:40
  140.7 50.2 %all-gather.7.cloned.1.call-done = bf16[1,2,1024,1024]{3,2,1,0:T(8,128)(2,1)} async-done(((bf16[1,2,1024,256]{3,2,1,0:T(8,128)(2,1)}), bf16[1,2,1024,1024]{3,2,1,0:T(8,128)(2,1)}) %all-gather.7.cloned.1.call-update) | async-done | bytes 4194320 | tf_op jit(solution)/shard_map/all_gather | solution.py:58
  190.9 9.9 %fusion.12 = bf16[2,1024,256]{2,1,0:T(8,128)(2,1)S(1)} fusion(bf16[2,1024,1024]{2,1,0:T(8,128)(2,1)} %bitcast.65, bf16[1,2,1024,1024]{3,2,1,0:T(8,128)(2,1)} %all-gather.7.cloned.1.call-done, bf16[1,2,1024,256]{3,2,1,0:T(8,128)(2,1)S(1)} %copy-done), kind=kOutput, calls=%fused_computation.14 | convolution fusion | flops 5371330560 | bytes 10485760 | tf_op jit(solution)/shard_map/sik,skj->sij/dot_general | solution.py:62
  200.7 2.1 copy.43
  202.8 12.1 %all-to-all-start.2 = ((bf16[2,1024,256]{2,0,1:T(2,128)(2,1)}), bf16[2,1024,256]{2,0,1:T(2,128)(2,1)S(1)}, u32[]{:S(2)}, u32[]{:S(2)}) async-start(bf16[2,1024,256]{2,0,1:T(2,128)(2,1)} %copy.43), calls=%async_computation.2 | async-start | bytes 2097152 | tf_op jit(solution)/shard_map/all_to_all | solution.py:65
  215.1 0.2 compare_reduce_fusion
  215.5 6.4 %fusion.5 = f32[1,2,1024,256]{3,2,1,0:T(8,128)} fusion(f32[1,2,1024,256]{3,2,1,0:T(8,128)} %param.9, bf16[2,1024,1024]{2,1,0:T(8,128)(2,1)} %bitcast.66, s32[]{:T(128)S(6)} %select_n.55, pred[2]{0:T(512)(128)(4,1)S(1)} %compare_reduce_fusion), kind=kOutput, calls=%fused_computation.9 | convolution fusion | flops 1075838976 | bytes 9437190 | tf_op jit(solution)/shard_map/ski,skj->sij/dot_general | solution.py:46
  221.9 2.8 %fusion.7 = f32[1,2,1024,256]{3,2,1,0:T(8,128)} fusion(f32[1,2,1024,256]{3,2,1,0:T(8,128)S(1)} %copy-done.3, bf16[2,1024,1024]{2,1,0:T(8,128)(2,1)S(1)} %bitcast.67, s32[]{:T(128)S(6)} %select_n.55, pred[2]{0:T(512)(128)(4,1)S(1)} %compare_reduce_fusion), kind=kOutput, calls=%fused_computation.13 | convolution fusion | flops 1075838976 | bytes 9437700 | tf_op jit(solution)/shard_map/sik,sjk->sij/dot_general | solution.py:45
  224.7 18.3 %all-to-all-done.2 = bf16[2,1024,256]{2,0,1:T(2,128)(2,1)S(1)} async-done(((bf16[2,1024,256]{2,0,1:T(2,128)(2,1)}), bf16[2,1024,256]{2,0,1:T(2,128)(2,1)S(1)}, u32[]{:S(2)}, u32[]{:S(2)}) %all-to-all-start.2) | async-done | bytes 1048608 | tf_op jit(solution)/shard_map/all_to_all | solution.py:65
  243.0 0.1 copy.44
  243.3 0.6 gather_fusion.1
  243.9 0.9 broadcast_select_fusion
  (27 shorter events, 1.1 us)
Async XLA Ops:
  7.2 183.7 %copy-start = (bf16[1,2,1024,256]{3,2,1,0:T(8,128)(2,1)S(1)}, bf16[1,2,1024,256]{3,2,1,0:T(8,128)(2,1)}, u32[]{:S(2)}) copy-start(bf16[1,2,1024,256]{3,2,1,0:T(8,128)(2,1)} %param.11) | copy-start | bytes 3145732
  12.2 5.0 %copy-start.2 = (s32[64,2]{0,1:T(2,128)S(1)}, s32[64,2]{0,1:T(2,128)}, u32[]{:S(2)}) copy-start(s32[64,2]{0,1:T(2,128)} %param.7) | copy-start | bytes 1540
  12.2 29.4 %all-to-all-start = ((bf16[4,64,16,256]{3,2,1,0:T(8,128)(2,1)}), bf16[4,64,16,256]{3,2,1,0:T(8,128)(2,1)S(1)}, u32[]{:S(2)}, u32[]{:S(2)}) async-start(bf16[4,64,16,256]{3,2,1,0:T(8,128)(2,1)} %copy.35), calls=%async_computation | async-start | bytes 4194304 | tf_op jit(solution)/shard_map/all_to_all | solution.py:17
  17.2 118.8 %all-gather.5.cloned.1.call-start = ((), (), s32[]{:S(2)}) async-start(), calls=%async_computation.3 | async-start | bytes 5242880 | tf_op jit(solution)/shard_map/all_gather | solution.py:40
  90.2 100.7 %all-gather.7.cloned.1.call-start = ((), (), s32[]{:S(2)}) async-start(), calls=%async_computation.4 | async-start | bytes 5242880 | tf_op jit(solution)/shard_map/all_gather | solution.py:58
  202.8 40.2 %all-to-all-start.2 = ((bf16[2,1024,256]{2,0,1:T(2,128)(2,1)}), bf16[2,1024,256]{2,0,1:T(2,128)(2,1)S(1)}, u32[]{:S(2)}, u32[]{:S(2)}) async-start(bf16[2,1024,256]{2,0,1:T(2,128)(2,1)} %copy.43), calls=%async_computation.2 | async-start | bytes 2097152 | tf_op jit(solution)/shard_map/all_to_all | solution.py:65
  215.4 6.5 %copy-start.1 = (bf16[4,2,128,8,256]{4,3,0,2,1:T(8,128)(2,1)S(1)}, bf16[4,2,128,8,256]{4,3,0,2,1:T(8,128)(2,1)}, u32[]{:S(2)}) copy-start(bf16[4,2,128,8,256]{4,3,0,2,1:T(8,128)(2,1)} %copy.49) | copy-start | bytes 12582916
  215.5 6.5 %copy-start.3 = (f32[1,2,1024,256]{3,2,1,0:T(8,128)S(1)}, f32[1,2,1024,256]{3,2,1,0:T(8,128)}, u32[]{:S(2)}) copy-start(f32[1,2,1024,256]{3,2,1,0:T(8,128)} %param.8) | copy-start | bytes 6291460
Sparse Core Ops, SparseCore 0:
  90.3 45.6 all-gather.4
  137.8 53.0 all-gather.6
